TPU v7x, 128 devices: a 2x2x16 block of a 8x8x16 slice. The times are simulated.
128 devices in a mesh: groups: 4 (over x, y), seq: 32 (over z, core).
Axes of the slice: x: 2, y: 2, z: 16, core: 2. Of those that a mesh axis runs over, the one named last changes fastest.
The devices are a block of a 8x8x16 slice.
Arguments:
- prefill_keys: bfloat16 [256, 8192, 128], P(('groups', 'seq')), parts along dimension 0, may hold values from -4 to 4
- prefill_values: bfloat16 [256, 8192, 128], P(('groups', 'seq')), parts along dimension 0, may hold values from -6 to 6
- window_queries: bfloat16 [256, 8, 256, 128], P(('groups', 'seq')), parts along dimension 0, may hold values from -48 to 48
- step_queries: bfloat16 [256, 2, 8, 128], P('groups'), parts along dimension 0, may hold values from -48 to 48
- new_keys: bfloat16 [256, 2, 128], P('groups'), parts along dimension 0, may hold values from -24 to 24
- new_values: bfloat16 [256, 2, 128], P('groups'), parts along dimension 0, may hold values from -6 to 6
- lengths: int32 [32], P('groups'), parts along dimension 0, may hold values from 4096 to 8192
- keep_mask: int32 [32, 64], P('groups'), parts along dimension 0, may hold values from 0 to 1, as said below
Outputs:
- cache_keys: bfloat16 [256, 8192, 128], P('groups', 'seq'), parts along dimension 0
- cache_values: bfloat16 [256, 8192, 128], P('groups', 'seq'), parts along dimension 0
- attended: bfloat16 [256, 2, 8, 128], P('groups'), parts along dimension 0
- block_scores: float32 [256, 64], P('groups', 'seq'), parts along dimension 0
There are 4 independent parts, one for each index of `groups`. A program takes and returns all parts, laid end to end along the dimension named above; each array names one. Nothing has to cross between parts.
Inputs may be any that keep to these rules, and one draw needn't show every extreme that they name: `keep_mask`: 1 keeps a block, 0 drops it; block 0 of every sequence is kept.
All inputs are finite; a program needn't handle non-finite values.
Results may differ from a plain program's by a relative error of at most 0.0055.
Values may be sent and summed in bfloat16 or wider, within the bound.
A program may use at most 128 MiB of HBM per device.

v0:
```python
import math

import jax
import jax.numpy as jnp
from jax import lax
from jax.sharding import PartitionSpec as P

KVH = 8
GROUP = 8
BLOCK = 128


def joined_along(pieces, dim):
    lengths = list(pieces.shape[1:])
    lengths[dim] *= pieces.shape[0]
    return jnp.moveaxis(pieces, 0, dim).reshape(lengths)


def copy_for_each(x, axis):
    copies = jnp.broadcast_to(x, (lax.axis_size(axis), *x.shape))
    return lax.all_to_all(copies, axis, split_axis=0, concat_axis=0, tiled=True)


def gather_directly(x, axis, dim):
    return joined_along(copy_for_each(x, axis), dim)


def window_mass(prefill_keys, window_queries, lengths, keep_mask, first_pair):
    pair_count, token_count, head_width = prefill_keys.shape
    block_count = keep_mask.shape[1]
    window_size = window_queries.shape[2]
    rows_pair = window_queries.shape[1] * window_size
    rows_block = math.gcd(rows_pair, 512)
    per_pair = rows_pair // rows_block
    flat_rows = window_queries.reshape(pair_count * per_pair, rows_block, head_width)
    scaling = 1.0 / math.sqrt(head_width)
    position = jnp.arange(token_count, dtype=jnp.int32)

    def one_block(block_index):
        pair_local = block_index // per_pair
        seq_id = (first_pair + pair_local) // KVH
        scores = (
            lax.dot_general(
                flat_rows[block_index],
                prefill_keys[pair_local],
                (((1,), (1,)), ((), ())),
                preferred_element_type=jnp.float32,
            )
            * scaling
        )
        row_offset = block_index % per_pair * rows_block + jnp.arange(rows_block, dtype=jnp.int32)
        query_pos = lengths[seq_id] - window_size + row_offset % window_size
        kept_tokens = jnp.broadcast_to(
            keep_mask[seq_id][:, None] > 0, (block_count, BLOCK)
        ).reshape(token_count)
        visible = kept_tokens[None, :] & (position[None, :] <= query_pos[:, None])
        scores = jnp.where(visible, scores, -jnp.inf)
        highest = jnp.max(scores, axis=1, keepdims=True)
        weights = jnp.exp(scores - highest)
        probability = weights / jnp.sum(weights, axis=1, keepdims=True)
        return jnp.sum(probability, axis=0).reshape(block_count, BLOCK).sum(axis=1)

    block_parts = lax.map(one_block, jnp.arange(pair_count * per_pair, dtype=jnp.int32))
    return block_parts.reshape(pair_count, per_pair, block_count).sum(axis=1) / GROUP


def select_rows(small_table, seq_ids):
    matches = seq_ids[:, None] == jnp.arange(small_table.shape[0], dtype=jnp.int32)[None, :]
    return jnp.sum(jnp.where(matches[:, :, None], small_table[None, :, :], 0), axis=1)


def step_scores(cache_part, queries_here, new_here, lengths, keep_mask, first_pair):
    pair_count, token_count, head_width = cache_part.shape
    step_count = queries_here.shape[1]
    group_size = queries_here.shape[2]
    query_rows = queries_here.reshape(pair_count, step_count * group_size, head_width)
    scaling = 1.0 / math.sqrt(head_width)
    scores = (
        jnp.einsum("pqd,ptd->pqt", query_rows, cache_part, preferred_element_type=jnp.float32)
        * scaling
    )
    seq_ids = (first_pair + jnp.arange(pair_count, dtype=jnp.int32)) // KVH
    block_count = token_count // BLOCK
    kept_blocks = select_rows(keep_mask, seq_ids) > 0
    kept_tokens = jnp.broadcast_to(
        kept_blocks[:, :, None], (pair_count, block_count, BLOCK)
    ).reshape(pair_count, token_count)
    seq_length = select_rows(lengths[:, None], seq_ids)[:, 0]
    position = jnp.arange(token_count, dtype=jnp.int32)
    visible = kept_tokens & (position[None, :] < seq_length[:, None])
    scores = jnp.where(visible[:, None, :], scores, -jnp.inf)
    own_scores = (
        jnp.einsum("pqd,pjd->pqj", query_rows, new_here, preferred_element_type=jnp.float32)
        * scaling
    )
    row_step = jnp.arange(step_count * group_size, dtype=jnp.int32) // group_size
    own_visible = jnp.arange(step_count, dtype=jnp.int32)[None, :] <= row_step[:, None]
    own_scores = jnp.where(own_visible[None], own_scores, -jnp.inf)
    return (scores, own_scores)


def local_terms(scores, cache_vals, highest):
    weights = jnp.exp(scores - highest[:, :, None])
    total_mass = jnp.sum(weights, axis=2)
    summed = jnp.einsum(
        "pqt,ptd->pqd", weights.astype(jnp.bfloat16), cache_vals, preferred_element_type=jnp.float32
    )
    return (weights, total_mass, summed)


def finish(summed, total_mass, weights, highest, own_scores, new_vals):
    own_weights = jnp.exp(own_scores - highest[:, :, None])
    total_mass = total_mass + jnp.sum(own_weights, axis=2)
    summed = summed + jnp.einsum(
        "pqj,pjd->pqd",
        own_weights.astype(jnp.bfloat16),
        new_vals,
        preferred_element_type=jnp.float32,
    )
    pair_count, row_count, head_width = summed.shape
    attended = (
        (summed / total_mass[:, :, None])
        .astype(jnp.bfloat16)
        .reshape(pair_count, row_count // GROUP, GROUP, head_width)
    )
    token_count = weights.shape[2]
    new_mass = (
        jnp.sum(weights / total_mass[:, :, None], axis=1)
        .reshape(pair_count, token_count // BLOCK, BLOCK)
        .sum(axis=2)
        / GROUP
    )
    return (attended, new_mass)


def local(
    prefill_keys,
    prefill_values,
    window_queries,
    step_queries,
    new_keys,
    new_values,
    lengths,
    keep_mask,
):
    pair_count = prefill_keys.shape[0]
    first_pair = lax.axis_index("seq") * pair_count
    prior_mass = window_mass(prefill_keys, window_queries, lengths, keep_mask, first_pair).astype(
        jnp.bfloat16
    )
    cache_keys, cache_values, prior_tokens = (
        lax.all_to_all(prefill_keys, "seq", split_axis=1, concat_axis=0, tiled=True),
        lax.all_to_all(prefill_values, "seq", split_axis=1, concat_axis=0, tiled=True),
        lax.all_to_all(prior_mass, "seq", split_axis=1, concat_axis=0, tiled=True),
    )
    queries_here = lax.dynamic_slice_in_dim(step_queries, first_pair, pair_count, 0)
    new_keys_here = lax.dynamic_slice_in_dim(new_keys, first_pair, pair_count, 0)
    new_values_here = lax.dynamic_slice_in_dim(new_values, first_pair, pair_count, 0)
    scores, own_scores = step_scores(
        prefill_keys, queries_here, new_keys_here, lengths, keep_mask, first_pair
    )
    highest = jnp.maximum(jnp.max(scores, axis=2), jnp.max(own_scores, axis=2))
    weights, total_mass, summed = local_terms(scores, prefill_values, highest)
    attended_here, mass_here = finish(
        summed, total_mass, weights, highest, own_scores, new_values_here
    )
    attended = gather_directly(attended_here, "seq", 0)
    new_mass = lax.all_to_all(mass_here, "seq", split_axis=1, concat_axis=0, tiled=True)
    block_scores = prior_tokens.astype(jnp.float32) + new_mass
    return (cache_keys, cache_values, attended, block_scores)


def solution(mesh):
    placed = (
        P(("groups", "seq"), None, None),
        P(("groups", "seq"), None, None),
        P(("groups", "seq"), None, None, None),
        P("groups", None, None, None),
        P("groups", None, None),
        P("groups", None, None),
        P("groups"),
        P("groups", None),
    )
    return jax.shard_map(
        local,
        mesh=mesh,
        in_specs=placed,
        out_specs=(
            P("groups", "seq", None),
            P("groups", "seq", None),
            P("groups", None, None, None),
            P("groups", "seq"),
        ),
        check_vma=False,
    )
```

profile of v0, /device:TPU:324, one launch (start us, length us, event | category | flops | bytes accessed | tf_op | source)
XLA Modules:
  0.0 757.9 jit_solution(12316995600203130622)
XLA Ops:
  0.7 283.6 %while.14 = (s32[]{:T(128)}, f32[8,64]{1,0:T(8,128)S(1)}, s32[8]{0:T(128)S(1)}, s32[]{:T(128)}, s32[8,64]{1,0:T(8,128)}, /*index=5*/s32[8]{0:T(128)}, bf16[8,512...) while((s32[]{:T(128)}, f32[8,64]{1,0:T(8,128)S(1)}, ...), condition=%wide.region_11.12_spmd.clone, body=%wide.region_6.11_spmd.clone.sunk | while | flops 1115690496 | bytes 52657964 | solution.py:63
  7.9 12.4 %fusion.44 = (f32[512]{0:T(512)S(1)}, f32[512,8192]{1,0:T(8,128)}) fusion(bf16[2,8192,128]{2,1,0:T(8,128)(2,1)} %get-tuple-element.299, s32[]{:T(128)S(6)} %select_n.157, bf16[8,512,128]{2,1,0:T(8,128)(2,1)} %get-tuple-element.298, s32[]{:T(128)S(6)} %select_n.158, s32[512]{0:T(512)S(1)} %fusion.43, pred[8192]{0:T(1024)(128)(4,1)S(1)} %broadcast_bitcast_fusion.3), kind=kOutput, calls=%fused_computation.68.clone.1 | convolution fusion | flops 1094712832 | bytes 19017736 | tf_op jit(solution)/shard_map/while/body/eval_jaxpr/dot_general | solution.py:43
  20.3 8.1 %fusion.45 = f32[512]{0:T(512)S(1)} fusion(f32[512,8192]{1,0:T(8,128)} %get-tuple-element.254, f32[512]{0:T(512)S(1)} %get-tuple-element.255), kind=kLoop, calls=%fused_computation.6.clone.1 | loop fusion | flops 8388096 | bytes 16781312 | tf_op jit(solution)/shard_map/while/body/eval_jaxpr/reduce_sum | solution.py:60
  28.4 7.5 divide_reduce_fusion.3
  43.3 12.4 %fusion.44 = (f32[512]{0:T(512)S(1)}, f32[512,8192]{1,0:T(8,128)}) fusion(bf16[2,8192,128]{2,1,0:T(8,128)(2,1)} %get-tuple-element.299, s32[]{:T(128)S(6)} %select_n.157, bf16[8,512,128]{2,1,0:T(8,128)(2,1)} %get-tuple-element.298, s32[]{:T(128)S(6)} %select_n.158, s32[512]{0:T(512)S(1)} %fusion.43, pred[8192]{0:T(1024)(128)(4,1)S(1)} %broadcast_bitcast_fusion.3), kind=kOutput, calls=%fused_computation.68.clone.1 | convolution fusion | flops 1094712832 | bytes 19017736 | tf_op jit(solution)/shard_map/while/body/eval_jaxpr/dot_general | solution.py:43
  55.8 8.1 %fusion.45 = f32[512]{0:T(512)S(1)} fusion(f32[512,8192]{1,0:T(8,128)} %get-tuple-element.254, f32[512]{0:T(512)S(1)} %get-tuple-element.255), kind=kLoop, calls=%fused_computation.6.clone.1 | loop fusion | flops 8388096 | bytes 16781312 | tf_op jit(solution)/shard_map/while/body/eval_jaxpr/reduce_sum | solution.py:60
  63.9 7.5 divide_reduce_fusion.3
  78.8 12.4 %fusion.44 = (f32[512]{0:T(512)S(1)}, f32[512,8192]{1,0:T(8,128)}) fusion(bf16[2,8192,128]{2,1,0:T(8,128)(2,1)} %get-tuple-element.299, s32[]{:T(128)S(6)} %select_n.157, bf16[8,512,128]{2,1,0:T(8,128)(2,1)} %get-tuple-element.298, s32[]{:T(128)S(6)} %select_n.158, s32[512]{0:T(512)S(1)} %fusion.43, pred[8192]{0:T(1024)(128)(4,1)S(1)} %broadcast_bitcast_fusion.3), kind=kOutput, calls=%fused_computation.68.clone.1 | convolution fusion | flops 1094712832 | bytes 19017736 | tf_op jit(solution)/shard_map/while/body/eval_jaxpr/dot_general | solution.py:43
  91.2 8.1 %fusion.45 = f32[512]{0:T(512)S(1)} fusion(f32[512,8192]{1,0:T(8,128)} %get-tuple-element.254, f32[512]{0:T(512)S(1)} %get-tuple-element.255), kind=kLoop, calls=%fused_computation.6.clone.1 | loop fusion | flops 8388096 | bytes 16781312 | tf_op jit(solution)/shard_map/while/body/eval_jaxpr/reduce_sum | solution.py:60
  99.3 7.5 divide_reduce_fusion.3
  114.2 12.4 %fusion.44 = (f32[512]{0:T(512)S(1)}, f32[512,8192]{1,0:T(8,128)}) fusion(bf16[2,8192,128]{2,1,0:T(8,128)(2,1)} %get-tuple-element.299, s32[]{:T(128)S(6)} %select_n.157, bf16[8,512,128]{2,1,0:T(8,128)(2,1)} %get-tuple-element.298, s32[]{:T(128)S(6)} %select_n.158, s32[512]{0:T(512)S(1)} %fusion.43, pred[8192]{0:T(1024)(128)(4,1)S(1)} %broadcast_bitcast_fusion.3), kind=kOutput, calls=%fused_computation.68.clone.1 | convolution fusion | flops 1094712832 | bytes 19017736 | tf_op jit(solution)/shard_map/while/body/eval_jaxpr/dot_general | solution.py:43
  126.7 8.1 %fusion.45 = f32[512]{0:T(512)S(1)} fusion(f32[512,8192]{1,0:T(8,128)} %get-tuple-element.254, f32[512]{0:T(512)S(1)} %get-tuple-element.255), kind=kLoop, calls=%fused_computation.6.clone.1 | loop fusion | flops 8388096 | bytes 16781312 | tf_op jit(solution)/shard_map/while/body/eval_jaxpr/reduce_sum | solution.py:60
  149.7 12.4 %fusion.44 = (f32[512]{0:T(512)S(1)}, f32[512,8192]{1,0:T(8,128)}) fusion(bf16[2,8192,128]{2,1,0:T(8,128)(2,1)} %get-tuple-element.299, s32[]{:T(128)S(6)} %select_n.157, bf16[8,512,128]{2,1,0:T(8,128)(2,1)} %get-tuple-element.298, s32[]{:T(128)S(6)} %select_n.158, s32[512]{0:T(512)S(1)} %fusion.43, pred[8192]{0:T(1024)(128)(4,1)S(1)} %broadcast_bitcast_fusion.3), kind=kOutput, calls=%fused_computation.68.clone.1 | convolution fusion | flops 1094712832 | bytes 19017736 | tf_op jit(solution)/shard_map/while/body/eval_jaxpr/dot_general | solution.py:43
  162.1 8.1 %fusion.45 = f32[512]{0:T(512)S(1)} fusion(f32[512,8192]{1,0:T(8,128)} %get-tuple-element.254, f32[512]{0:T(512)S(1)} %get-tuple-element.255), kind=kLoop, calls=%fused_computation.6.clone.1 | loop fusion | flops 8388096 | bytes 16781312 | tf_op jit(solution)/shard_map/while/body/eval_jaxpr/reduce_sum | solution.py:60
  170.2 7.5 divide_reduce_fusion.3
  185.1 12.4 %fusion.44 = (f32[512]{0:T(512)S(1)}, f32[512,8192]{1,0:T(8,128)}) fusion(bf16[2,8192,128]{2,1,0:T(8,128)(2,1)} %get-tuple-element.299, s32[]{:T(128)S(6)} %select_n.157, bf16[8,512,128]{2,1,0:T(8,128)(2,1)} %get-tuple-element.298, s32[]{:T(128)S(6)} %select_n.158, s32[512]{0:T(512)S(1)} %fusion.43, pred[8192]{0:T(1024)(128)(4,1)S(1)} %broadcast_bitcast_fusion.3), kind=kOutput, calls=%fused_computation.68.clone.1 | convolution fusion | flops 1094712832 | bytes 19017736 | tf_op jit(solution)/shard_map/while/body/eval_jaxpr/dot_general | solution.py:43
  197.6 8.1 %fusion.45 = f32[512]{0:T(512)S(1)} fusion(f32[512,8192]{1,0:T(8,128)} %get-tuple-element.254, f32[512]{0:T(512)S(1)} %get-tuple-element.255), kind=kLoop, calls=%fused_computation.6.clone.1 | loop fusion | flops 8388096 | bytes 16781312 | tf_op jit(solution)/shard_map/while/body/eval_jaxpr/reduce_sum | solution.py:60
  220.6 12.4 %fusion.44 = (f32[512]{0:T(512)S(1)}, f32[512,8192]{1,0:T(8,128)}) fusion(bf16[2,8192,128]{2,1,0:T(8,128)(2,1)} %get-tuple-element.299, s32[]{:T(128)S(6)} %select_n.157, bf16[8,512,128]{2,1,0:T(8,128)(2,1)} %get-tuple-element.298, s32[]{:T(128)S(6)} %select_n.158, s32[512]{0:T(512)S(1)} %fusion.43, pred[8192]{0:T(1024)(128)(4,1)S(1)} %broadcast_bitcast_fusion.3), kind=kOutput, calls=%fused_computation.68.clone.1 | convolution fusion | flops 1094712832 | bytes 19017736 | tf_op jit(solution)/shard_map/while/body/eval_jaxpr/dot_general | solution.py:43
  233.0 8.1 %fusion.45 = f32[512]{0:T(512)S(1)} fusion(f32[512,8192]{1,0:T(8,128)} %get-tuple-element.254, f32[512]{0:T(512)S(1)} %get-tuple-element.255), kind=kLoop, calls=%fused_computation.6.clone.1 | loop fusion | flops 8388096 | bytes 16781312 | tf_op jit(solution)/shard_map/while/body/eval_jaxpr/reduce_sum | solution.py:60
  241.1 7.5 divide_reduce_fusion.3
  256.0 12.4 %fusion.44 = (f32[512]{0:T(512)S(1)}, f32[512,8192]{1,0:T(8,128)}) fusion(bf16[2,8192,128]{2,1,0:T(8,128)(2,1)} %get-tuple-element.299, s32[]{:T(128)S(6)} %select_n.157, bf16[8,512,128]{2,1,0:T(8,128)(2,1)} %get-tuple-element.298, s32[]{:T(128)S(6)} %select_n.158, s32[512]{0:T(512)S(1)} %fusion.43, pred[8192]{0:T(1024)(128)(4,1)S(1)} %broadcast_bitcast_fusion.3), kind=kOutput, calls=%fused_computation.68.clone.1 | convolution fusion | flops 1094712832 | bytes 19017736 | tf_op jit(solution)/shard_map/while/body/eval_jaxpr/dot_general | solution.py:43
  268.4 8.1 %fusion.45 = f32[512]{0:T(512)S(1)} fusion(f32[512,8192]{1,0:T(8,128)} %get-tuple-element.254, f32[512]{0:T(512)S(1)} %get-tuple-element.255), kind=kLoop, calls=%fused_computation.6.clone.1 | loop fusion | flops 8388096 | bytes 16781312 | tf_op jit(solution)/shard_map/while/body/eval_jaxpr/reduce_sum | solution.py:60
  285.0 16.3 %all-to-all-start.3 = ((bf16[2,32,2]{2,0,1:T(2,128)(2,1)}), bf16[2,32,2]{2,0,1:T(2,128)(2,1)S(1)}, u32[]{:S(2)}, u32[]{:S(2)}) async-start(bf16[2,32,2]{2,0,1:T(2,128)(2,1)} %copy.29), calls=%async_computation.3 | async-start | bytes 32768 | tf_op jit(solution)/shard_map/all_to_all | solution.py:154
  311.5 11.3 %all-to-all-start.4 = ((f32[2,32,2]{2,0,1:T(2,128)}), f32[2,32,2]{2,0,1:T(2,128)S(1)}, u32[]{:S(2)}, u32[]{:S(2)}) async-start(f32[2,32,2]{2,0,1:T(2,128)} %copy.30), calls=%async_computation.4 | async-start | bytes 65536 | tf_op jit(solution)/shard_map/all_to_all | solution.py:168
  323.6 9.6 %all-to-all-done.4 = f32[2,32,2]{2,0,1:T(2,128)S(1)} async-done(((f32[2,32,2]{2,0,1:T(2,128)}), f32[2,32,2]{2,0,1:T(2,128)S(1)}, u32[]{:S(2)}, u32[]{:S(2)}) %all-to-all-start.4) | async-done | bytes 544 | tf_op jit(solution)/shard_map/all_to_all | solution.py:168
  340.3 10.1 %copy.27 = bf16[2,8192,128]{2,0,1:T(2,128)(2,1)} copy(bf16[2,8192,128]{2,1,0:T(8,128)(2,1)} %param.11) | data formatting | bytes 8388608 | tf_op args[1]
  350.4 8.9 %all-to-all-done.2 = bf16[32,2,2,8,128]{4,3,2,1,0:T(8,128)(2,1)S(1)} async-done(((bf16[32,2,2,8,128]{4,3,2,1,0:T(8,128)(2,1)}), bf16[32,2,2,8,128]{4,3,2,1,0:T(8,128)(2,1)S(1)}, u32[]{:S(2)}, u32[]{:S(2)}) %all-to-all-start.2) | async-done | bytes 262176 | tf_op jit(solution)/shard_map/all_to_all | solution.py:21
  359.3 8.6 %all-to-all-start.1 = ((bf16[2,8192,128]{2,0,1:T(2,128)(2,1)}), bf16[2,8192,128]{2,0,1:T(2,128)(2,1)}, u32[]{:S(2)}, u32[]{:S(2)}) async-start(bf16[2,8192,128]{2,0,1:T(2,128)(2,1)} %copy.27), calls=%async_computation.1 | async-start | bytes 8388608 | tf_op jit(solution)/shard_map/all_to_all | solution.py:153
  367.9 10.1 %copy.25 = bf16[2,8192,128]{2,0,1:T(2,128)(2,1)} copy(bf16[2,8192,128]{2,1,0:T(8,128)(2,1)} %get-tuple-element.318) | data formatting | bytes 8388608 | tf_op args[0]
  378.0 177.6 %all-to-all-done.1 = bf16[2,8192,128]{2,0,1:T(2,128)(2,1)} async-done(((bf16[2,8192,128]{2,0,1:T(2,128)(2,1)}), bf16[2,8192,128]{2,0,1:T(2,128)(2,1)}, u32[]{:S(2)}, u32[]{:S(2)}) %all-to-all-start.1) | async-done | bytes 4194336 | tf_op jit(solution)/shard_map/all_to_all | solution.py:153
  555.6 8.6 %all-to-all-start = ((bf16[2,8192,128]{2,0,1:T(2,128)(2,1)}), bf16[2,8192,128]{2,0,1:T(2,128)(2,1)}, u32[]{:S(2)}, u32[]{:S(2)}) async-start(bf16[2,8192,128]{2,0,1:T(2,128)(2,1)} %copy.25), calls=%async_computation | async-start | bytes 8388608 | tf_op jit(solution)/shard_map/all_to_all | solution.py:152
  570.2 181.7 %all-to-all-done = bf16[2,8192,128]{2,0,1:T(2,128)(2,1)} async-done(((bf16[2,8192,128]{2,0,1:T(2,128)(2,1)}), bf16[2,8192,128]{2,0,1:T(2,128)(2,1)}, u32[]{:S(2)}, u32[]{:S(2)}) %all-to-all-start) | async-done | bytes 4194336 | tf_op jit(solution)/shard_map/all_to_all | solution.py:152
  (99 shorter events, 75.3 us)
Async XLA Ops:
  0.6 302.7 %copy-start = (bf16[64,2,8,128]{3,2,1,0:T(8,128)(2,1)S(1)}, bf16[64,2,8,128]{3,2,1,0:T(8,128)(2,1)}, u32[]{:S(2)}) copy-start(bf16[64,2,8,128]{3,2,1,0:T(8,128)(2,1)} %param.13) | copy-start | bytes 786436
  285.0 26.5 %all-to-all-start.3 = ((bf16[2,32,2]{2,0,1:T(2,128)(2,1)}), bf16[2,32,2]{2,0,1:T(2,128)(2,1)S(1)}, u32[]{:S(2)}, u32[]{:S(2)}) async-start(bf16[2,32,2]{2,0,1:T(2,128)(2,1)} %copy.29), calls=%async_computation.3 | async-start | bytes 32768 | tf_op jit(solution)/shard_map/all_to_all | solution.py:154
  303.2 5.0 copy-start.1
  311.5 21.7 %all-to-all-start.4 = ((f32[2,32,2]{2,0,1:T(2,128)}), f32[2,32,2]{2,0,1:T(2,128)S(1)}, u32[]{:S(2)}, u32[]{:S(2)}) async-start(f32[2,32,2]{2,0,1:T(2,128)} %copy.30), calls=%async_computation.4 | async-start | bytes 65536 | tf_op jit(solution)/shard_map/all_to_all | solution.py:168
  333.9 25.4 %all-to-all-start.2 = ((bf16[32,2,2,8,128]{4,3,2,1,0:T(8,128)(2,1)}), bf16[32,2,2,8,128]{4,3,2,1,0:T(8,128)(2,1)S(1)}, u32[]{:S(2)}, u32[]{:S(2)}) async-start(bf16[32,2,2,8,128]{4,3,2,1,0:T(8,128)(2,1)} %broadcast_in_dim.124), calls=%async_computation.2 | async-start | bytes 524288 | tf_op jit(solution)/shard_map/all_to_all | solution.py:21
  359.3 196.3 %all-to-all-start.1 = ((bf16[2,8192,128]{2,0,1:T(2,128)(2,1)}), bf16[2,8192,128]{2,0,1:T(2,128)(2,1)}, u32[]{:S(2)}, u32[]{:S(2)}) async-start(bf16[2,8192,128]{2,0,1:T(2,128)(2,1)} %copy.27), calls=%async_computation.1 | async-start | bytes 8388608 | tf_op jit(solution)/shard_map/all_to_all | solution.py:153
  555.6 196.3 %all-to-all-start = ((bf16[2,8192,128]{2,0,1:T(2,128)(2,1)}), bf16[2,8192,128]{2,0,1:T(2,128)(2,1)}, u32[]{:S(2)}, u32[]{:S(2)}) async-start(bf16[2,8192,128]{2,0,1:T(2,128)(2,1)} %copy.25), calls=%async_computation | async-start | bytes 8388608 | tf_op jit(solution)/shard_map/all_to_all | solution.py:152
where the time goes:
time: 765 us; the launch traced here: 758 us
  waiting for transfers between devices  379 us (50%)
  other arithmetic  134 us (18%)
  matrix products  106 us (14%)
  starting transfers between devices  51.3 us (7%)
  local copies, waits for them, and re-layouts  50 us (7%)
  loops' own time  37 us (5%)
    all_to_all x1, waiting for transfers between devices, local(): lax.all_to_all(prefill_keys, 'seq', split_axis=1, concat_axis=0, tiled=True)  182 us
    all_to_all x1, waiting for transfers between devices, local(): lax.all_to_all(prefill_values, 'seq', split_axis=1, concat_axis=0, tiled=...  178 us
    dot_general x8, matrix products, one_block(): lax.dot_general(flat_rows[block_index], prefill_keys[pair_local], (((1,),...  99.5 us
    reduce_sum x8, other arithmetic, one_block(): probability = weights / jnp.sum(weights, axis=1, keepdims=True)  64.9 us
    reduce_sum x16, other arithmetic, one_block(): return jnp.sum(probability, axis=0).reshape(block_count, BLOCK).sum(axis=1)  61.1 us
    another operation x1, loops' own time, window_mass(): lax.map(one_block, jnp.arange(pair_count * per_pair, dtype=jnp.int32))  37 us
    unnamed x8, local copies, waits for them, and re-layouts  21 us
    all_to_all x1, starting transfers between devices, local(): lax.all_to_all(prior_mass, 'seq', split_axis=1, concat_axis=0, tiled=True)  16.3 us
  transfers between devices with their start and end apart: 5, of which 5 were waited for; matrix products, arithmetic and copies ran while one was open for 5% of the time, Pallas kernels for 0%

commit v1 on v0

v1 whole, which is shorter than its diff:
```python
import functools
import math

import jax
import jax.numpy as jnp
from jax import lax
from jax.experimental import pallas as pl
from jax.experimental.pallas import tpu as pltpu
from jax.sharding import PartitionSpec as P

KVH = 8
GROUP = 8
BLOCK = 128
LOG2E = 1.4426950408889634
NEG = -1e30
MESH = pl.DeviceIdType.MESH


def remote(src, dst, send_sem, recv_sem, peer):
    return pltpu.make_async_remote_copy(
        src_ref=src,
        dst_ref=dst,
        send_sem=send_sem,
        recv_sem=recv_sem,
        device_id={"seq": peer},
        device_id_type=MESH,
    )


def main_kernel(
    n,
    k_hbm,
    v_hbm,
    wq_hbm,
    sq_hbm,
    nk_hbm,
    nv_hbm,
    lengths_hbm,
    keep_hbm,
    ck,
    cv,
    att,
    sco,
    kbuf,
    vbuf,
    wq,
    sq,
    nk,
    nv,
    lengths_ref,
    keep_smem,
    keep_vmem,
    logits,
    sbuf,
    mbuf,
    wbuf,
    acc,
    mass,
    column,
    message,
    load_sem,
    own_sem,
    send_sem,
    recv_sem,
    small_send,
    small_recv,
):
    pairs, tokens, width = kbuf.shape
    share = tokens // n
    blocks = tokens // BLOCK
    share_blocks = blocks // n
    window = wq.shape[2]
    rows = sq.shape[1]
    chips = n // 2
    me = lax.axis_index("seq")
    z, c = me // 2, me % 2
    first_pair = me * pairs
    seq_id = first_pair // KVH
    scaling = 1.0 / math.sqrt(width)
    fold = scaling * LOG2E

    barrier = pltpu.get_barrier_semaphore()
    for step in range(1, n):
        pl.semaphore_signal(
            barrier, inc=1, device_id={"seq": lax.rem(me + step, n)}, device_id_type=MESH
        )

    loads = [
        pltpu.make_async_copy(k_hbm, kbuf, load_sem.at[0]),
        pltpu.make_async_copy(sq_hbm.at[pl.ds(first_pair, pairs)], sq, load_sem.at[1]),
        pltpu.make_async_copy(nk_hbm.at[pl.ds(first_pair, pairs)], nk, load_sem.at[2]),
        pltpu.make_async_copy(nv_hbm.at[pl.ds(first_pair, pairs)], nv, load_sem.at[3]),
        pltpu.make_async_copy(lengths_hbm, lengths_ref, load_sem.at[4]),
        pltpu.make_async_copy(keep_hbm, keep_smem, load_sem.at[5]),
        pltpu.make_async_copy(keep_hbm, keep_vmem, load_sem.at[6]),
        pltpu.make_async_copy(v_hbm, vbuf, load_sem.at[7]),
        pltpu.make_async_copy(wq_hbm, wq, load_sem.at[8]),
    ]
    for load in loads:
        load.start()
    mine = pl.ds(first_pair, pairs)
    own = [
        pltpu.make_async_copy(
            src.at[:, pl.ds(pl.multiple_of(me * share, share), share), :], dst.at[mine], own_sem.at[i]
        )
        for i, (src, dst) in enumerate(((k_hbm, ck), (v_hbm, cv)))
    ]
    for copy in own:
        copy.start()

    pl.semaphore_wait(barrier, n - 1)

    def send_share(src, dst, i, first, last):
        def one(turn, carry):
            step = jnp.where(turn % 2 == 0, (turn + 1) // 2, n - (turn + 1) // 2)
            peer = lax.rem(me + step, n)
            remote(
                src.at[:, pl.ds(pl.multiple_of(peer * share, share), share), :],
                dst.at[mine],
                send_sem.at[i],
                recv_sem.at[i],
                peer,
            ).start()
            return carry

        lax.fori_loop(first, last, one, 0)

    send_share(k_hbm, ck, 0, 1, n)

    for load in loads[:8]:
        load.wait()
    length = lengths_ref[seq_id]
    chunk = 8 * BLOCK
    chunks = tokens // chunk
    for i in range(pairs):
        query = sq[i]
        lane = lax.broadcasted_iota(jnp.int32, (1, chunk), 1)

        def score_chunk(j, highest):
            base = pl.multiple_of(j * chunk, chunk)
            s = lax.dot_general(
                query,
                kbuf[i, pl.ds(base, chunk), :],
                (((1,), (1,)), ((), ())),
                preferred_element_type=jnp.float32,
            )
            kept = jnp.concatenate(
                [
                    jnp.full((1, BLOCK), keep_smem[seq_id, j * 8 + u], jnp.int32)
                    for u in range(8)
                ],
                axis=1,
            )
            limit = jnp.where(kept > 0, length, 0)
            s = jnp.where(lane + base < limit, s * scaling, NEG)
            logits[:, pl.ds(base, chunk)] = s
            return jnp.maximum(highest, jnp.max(s, axis=1, keepdims=True))

        highest = lax.fori_loop(0, chunks, score_chunk, jnp.full((rows, 1), NEG, jnp.float32))
        steps = nk.shape[1]
        query_f = query.astype(jnp.float32)
        row_step = lax.broadcasted_iota(jnp.int32, (rows, 1), 0) // GROUP
        own_scores = []
        for j in range(steps):
            key_f = nk[i].astype(jnp.float32)[j : j + 1]
            o = jnp.sum(query_f * key_f, axis=1, keepdims=True) * scaling
            o = jnp.where(row_step >= j, o, NEG)
            own_scores.append(o)
            highest = jnp.maximum(highest, o)
        own_weights = [jnp.exp(o - highest) for o in own_scores]
        extra_total = sum(own_weights)
        extra_sum = sum(
            w.astype(jnp.bfloat16).astype(jnp.float32) * nv[i].astype(jnp.float32)[j : j + 1]
            for j, w in enumerate(own_weights)
        )

        def value_chunk(j, carry):
            total, summed = carry
            base = pl.multiple_of(j * chunk, chunk)
            w = jnp.exp(logits[:, pl.ds(base, chunk)] - highest)
            logits[:, pl.ds(base, chunk)] = w
            total = total + jnp.sum(w, axis=1, keepdims=True)
            summed = summed + jnp.dot(
                w.astype(jnp.bfloat16),
                vbuf[i, pl.ds(base, chunk), :],
                preferred_element_type=jnp.float32,
            )
            return total, summed

        total, summed = lax.fori_loop(0, chunks, value_chunk, (extra_total, extra_sum))
        inverse = 1.0 / total
        result = (summed / total).astype(jnp.bfloat16)
        att[z // 4, z % 4, c, i] = result

        def mass_chunk(j, carry):
            base = pl.multiple_of(j * chunk, chunk)
            w = jnp.sum(logits[:, pl.ds(base, chunk)] * inverse, axis=0, keepdims=True)
            tile = jnp.concatenate([w[:, u * BLOCK : (u + 1) * BLOCK] for u in range(8)], axis=0)
            mass[i, pl.ds(pl.multiple_of(j * 8, 8), 8), :] = tile
            return carry

        lax.fori_loop(0, chunks, mass_chunk, 0)

    half = n // 2
    send_share(v_hbm, cv, 1, half, n)

    def chip(step):
        return lax.rem(z + step + chips, chips) * 2 + c

    slot = att.at[z // 4, z % 4, c]
    far = [
        remote(slot, slot, small_send.at[k], small_recv.at[k], chip(step))
        for k, step in enumerate((4, -4, 8))
    ]
    for copy in far:
        copy.start()

    loads[8].wait()
    eye = lax.broadcasted_iota(jnp.int32, (blocks, blocks), 0) == lax.broadcasted_iota(
        jnp.int32, (blocks, blocks), 1
    )
    keep_row = jnp.broadcast_to(keep_vmem[pl.ds(seq_id, 1), :], (blocks, blocks))
    keep_col = jnp.sum(jnp.where(eye, keep_row, 0), axis=1, keepdims=True) > 0
    limit_row = length - window + lax.broadcasted_iota(jnp.int32, (1, window), 1)
    token = lax.broadcasted_iota(jnp.int32, (BLOCK, BLOCK), 0)

    for i in range(pairs):
        acc[...] = jnp.zeros_like(acc)

        def one_group(g, carry):
            query = wq[i, g]

            def one_chunk(j, inner):
                base = pl.multiple_of(j * chunk, chunk)
                sbuf[...] = lax.dot_general(
                    kbuf[i, pl.ds(base, chunk), :],
                    query,
                    (((1,), (1,)), ((), ())),
                    preferred_element_type=jnp.float32,
                )
                here = pl.ds(pl.multiple_of(j * 8, 8), 8)
                for h in range(0, window, BLOCK):
                    tops, sums = [], []
                    for u in range(8):
                        s = sbuf[u * BLOCK : (u + 1) * BLOCK, h : h + BLOCK]
                        s = jnp.where(token <= limit_row[:, h : h + BLOCK] - (base + u * BLOCK), s, NEG)
                        m = jnp.max(s, axis=0, keepdims=True)
                        e = jnp.exp2((s - m) * fold)
                        tops.append(m)
                        sums.append(jnp.sum(e, axis=0, keepdims=True))
                    mbuf[here, h : h + BLOCK] = jnp.concatenate(tops, axis=0)
                    wbuf[here, h : h + BLOCK] = jnp.concatenate(sums, axis=0)
                return inner

            lax.fori_loop(0, chunks, one_chunk, 0)
            m = jnp.where(keep_col, mbuf[...], NEG)
            top = jnp.max(m, axis=0, keepdims=True)
            w = wbuf[...] * jnp.exp2((m - top) * fold)
            acc[...] += w / jnp.sum(w, axis=0, keepdims=True)
            return carry

        lax.fori_loop(0, wq.shape[1], one_group, 0)
        prior = jnp.sum(acc[...], axis=1, keepdims=True) / GROUP
        prior = prior.astype(jnp.bfloat16).astype(jnp.float32)
        new_mass = jnp.sum(mass[i], axis=1, keepdims=True) / GROUP
        column[i] = jnp.broadcast_to(prior + new_mass, (blocks, BLOCK))

    target = lax.broadcasted_iota(jnp.int32, (n, blocks), 0)
    source = lax.broadcasted_iota(jnp.int32, (n, blocks), 1)
    lanes = lax.broadcasted_iota(jnp.int32, (n, BLOCK), 1)
    table = jnp.zeros((n, BLOCK), jnp.float32)
    for i in range(pairs):
        value = column[i][:, :blocks]
        as_row = jnp.sum(jnp.where(eye, value, 0.0), axis=0, keepdims=True)
        for j in range(share_blocks):
            picked = jnp.where(source == target * share_blocks + j, as_row, 0.0)
            entry = jnp.sum(picked, axis=1, keepdims=True)
            table = jnp.where(lanes == i * share_blocks + j, entry, table)
    for d in range(n):
        message[d] = table[d : d + 1]

    for copy in far:
        copy.wait()
    line = att.at[:, z % 4, c]
    near = []
    for k, step in enumerate((1, -1, 2 - 4 * c)):
        near.append(remote(line, line, small_send.at[3 + k], small_recv.at[3 + k], chip(step)))
    for copy in near:
        copy.start()

    def send_scores(step, carry):
        peer = lax.rem(me + step, n)
        remote(message.at[peer], sco.at[me], small_send.at[7], small_recv.at[7], peer).start()
        return carry

    lax.fori_loop(1, n, send_scores, 0)
    keep_own = pltpu.make_async_copy(message.at[me], sco.at[me], own_sem.at[2])
    keep_own.start()

    send_share(v_hbm, cv, 1, 1, half)

    for copy in near:
        copy.wait()
    side = att.at[:, :, c]
    across = remote(side, side, small_send.at[6], small_recv.at[6], me + 1 - 2 * c)
    across.start()

    for copy in own:
        copy.wait()
    keep_own.wait()
    across.wait()
    others = pl.ds(0, (n - 1) * pairs)
    for i, dst in enumerate((ck, cv)):
        pltpu.make_async_copy(dst.at[others], dst.at[others], send_sem.at[i]).wait()
        pltpu.make_async_copy(dst.at[others], dst.at[others], recv_sem.at[i]).wait()
    peers = pl.ds(0, n - 1)
    pltpu.make_async_copy(sco.at[peers], sco.at[peers], small_send.at[7]).wait()
    pltpu.make_async_copy(sco.at[peers], sco.at[peers], small_recv.at[7]).wait()


def write_kernel(ck, cv, att, sco, ck_out, cv_out, att_out, bs_out, sems):
    copies = [
        pltpu.make_async_copy(src, dst, sems.at[i])
        for i, (src, dst) in enumerate(((ck, ck_out), (cv, cv_out), (att, att_out)))
    ]
    for copy in copies:
        copy.start()
    n = sco.shape[0]
    columns, rows = bs_out.shape
    pairs = rows // n
    table = jnp.concatenate([sco[s] for s in range(n)], axis=0)
    source = lax.broadcasted_iota(jnp.int32, (n, rows), 0)
    pair = lax.broadcasted_iota(jnp.int32, (n, rows), 1)
    for j in range(columns):
        total = jnp.zeros((1, rows), jnp.float32)
        for i in range(pairs):
            entry = table[:, i * columns + j : i * columns + j + 1]
            picked = jnp.where(pair == source * pairs + i, entry, 0.0)
            total = total + jnp.sum(picked, axis=0, keepdims=True)
        bs_out[j : j + 1, :] = total
    for copy in copies:
        copy.wait()


def local(
    n,
    prefill_keys,
    prefill_values,
    window_queries,
    step_queries,
    new_keys,
    new_values,
    lengths,
    keep_mask,
):
    pairs, tokens, width = prefill_keys.shape
    all_pairs, steps, group, _ = step_queries.shape
    share = tokens // n
    blocks = tokens // BLOCK
    rows = steps * group
    window = window_queries.shape[2]
    bf16, f32 = jnp.bfloat16, jnp.float32
    anywhere = pl.BlockSpec(memory_space=pl.ANY)
    att_shape = (4, n // 8, 2, pairs, rows, width)
    landed = pl.pallas_call(
        functools.partial(main_kernel, n),
        out_shape=[
            pltpu.VMEM((all_pairs, share, width), bf16),
            pltpu.VMEM((all_pairs, share, width), bf16),
            pltpu.VMEM(att_shape, bf16),
            pltpu.VMEM((n, 1, BLOCK), f32),
        ],
        in_specs=[anywhere] * 8,
        out_specs=[pl.BlockSpec(memory_space=pltpu.VMEM)] * 4,
        scratch_shapes=[
            pltpu.VMEM((pairs, tokens, width), bf16),
            pltpu.VMEM((pairs, tokens, width), bf16),
            pltpu.VMEM(window_queries.shape, bf16),
            pltpu.VMEM((pairs, rows, width), bf16),
            pltpu.VMEM((pairs, steps, width), bf16),
            pltpu.VMEM((pairs, steps, width), bf16),
            pltpu.SMEM(lengths.shape, jnp.int32),
            pltpu.SMEM(keep_mask.shape, jnp.int32),
            pltpu.VMEM(keep_mask.shape, jnp.int32),
            pltpu.VMEM((rows, tokens), f32),
            pltpu.VMEM((8 * BLOCK, window), f32),
            pltpu.VMEM((blocks, window), f32),
            pltpu.VMEM((blocks, window), f32),
            pltpu.VMEM((blocks, window), f32),
            pltpu.VMEM((pairs, blocks, BLOCK), f32),
            pltpu.VMEM((pairs, blocks, BLOCK), f32),
            pltpu.VMEM((n, 1, BLOCK), f32),
            pltpu.SemaphoreType.DMA((9,)),
            pltpu.SemaphoreType.DMA((3,)),
            pltpu.SemaphoreType.DMA((2,)),
            pltpu.SemaphoreType.DMA((2,)),
            pltpu.SemaphoreType.DMA((8,)),
            pltpu.SemaphoreType.DMA((8,)),
        ],
        compiler_params=pltpu.CompilerParams(
            collective_id=0, has_side_effects=True, vmem_limit_bytes=36 * 1024 * 1024
        ),
        name="exchange",
    )(
        *(
            pltpu.with_memory_space_constraint(x, pltpu.HBM)
            for x in (
                prefill_keys,
                prefill_values,
                window_queries,
                step_queries.reshape(all_pairs, rows, width),
                new_keys,
                new_values,
                lengths,
                keep_mask,
            )
        )
    )
    cache_keys, cache_values, attended, block_scores = pl.pallas_call(
        write_kernel,
        out_shape=[
            jax.ShapeDtypeStruct((all_pairs, share, width), bf16),
            jax.ShapeDtypeStruct((all_pairs, share, width), bf16),
            jax.ShapeDtypeStruct(att_shape, bf16),
            jax.ShapeDtypeStruct((blocks // n, all_pairs), f32),
        ],
        in_specs=[anywhere, anywhere, anywhere, pl.BlockSpec(memory_space=pltpu.VMEM)],
        out_specs=[anywhere, anywhere, anywhere, pl.BlockSpec(memory_space=pltpu.VMEM)],
        scratch_shapes=[pltpu.SemaphoreType.DMA((3,))],
        compiler_params=pltpu.CompilerParams(vmem_limit_bytes=4 * 1024 * 1024),
        name="write",
    )(*landed)
    return (
        cache_keys,
        cache_values,
        attended.reshape(all_pairs, steps, group, width),
        block_scores.T,
    )


def solution(mesh):
    placed = (
        P(("groups", "seq"), None, None),
        P(("groups", "seq"), None, None),
        P(("groups", "seq"), None, None, None),
        P("groups", None, None, None),
        P("groups", None, None),
        P("groups", None, None),
        P("groups"),
        P("groups", None),
    )
    return jax.shard_map(
        functools.partial(local, mesh.shape["seq"]),
        mesh=mesh,
        in_specs=placed,
        out_specs=(
            P("groups", "seq", None),
            P("groups", "seq", None),
            P("groups", None, None, None),
            P("groups", "seq"),
        ),
        check_vma=False,
    )
```

time: 765 us -> 395 us (0.52)
  Pallas kernels: 0 us -> 395 us
  waiting for transfers between devices: 379 us -> 0 us
  other arithmetic: 134 us -> 0 us
  matrix products: 106 us -> 0 us
  starting transfers between devices: 51.3 us -> 0 us
  local copies, waits for them, and re-layouts: 50 us -> 0 us
  loops' own time: 37 us -> 0 us
    pallas_call x0 -> x2, Pallas kernels: none -> 395 us  [the longest x1 391 us: local(): pl.pallas_call(functools.partial(main_kernel, n), out_shape=[pltpu.VMEM((...]
    all_to_all x5 -> x0, waiting for transfers between devices: 379 us -> none  [the longest x1 182 us: local(): lax.all_to_all(prefill_keys, 'seq', split_axis=1, concat_axis=0, tiled=True)]
    reduce_sum x31 -> x0, other arithmetic: 128 us -> none  [the longest x8 64.9 us: one_block(): probability = weights / jnp.sum(weights, axis=1, keepdims=True)]
    dot_general x12 -> x0, matrix products: 106 us -> none  [the longest x8 99.5 us: one_block(): lax.dot_general(flat_rows[block_index], prefill_keys[pair_local], (((1,),...]
    all_to_all x5 -> x0, starting transfers between devices: 51.3 us -> none  [the longest x1 16.3 us: local(): lax.all_to_all(prior_mass, 'seq', split_axis=1, concat_axis=0, tiled=True)]
    another operation x1 -> x0, loops' own time: 37 us -> none  [window_mass(): lax.map(one_block, jnp.arange(pair_count * per_pair, dtype=jnp.int32))]
    unnamed x8 -> x0, local copies, waits for them, and re-layouts: 21 us -> none
    dynamic_slice x16 -> x0, local copies, waits for them, and re-layouts: 14.6 us -> none  [the longest x8 9.94 us: one_block(): query_pos = lengths[seq_id] - window_size + row_offset % window_size]
  transfers between devices with their start and end apart: 5 -> 0, of which waited for: 5 -> 0; matrix products, arithmetic and copies ran while one was open for 5% -> 0% of each run, Pallas kernels for 0% -> 0%
where the time goes in v1:
time: 395 us
  Pallas kernels  395 us (100%)
    pallas_call x1, Pallas kernels, local(): pl.pallas_call(functools.partial(main_kernel, n), out_shape=[pltpu.VMEM((...  391 us

profile of v1, /device:TPU:324, one launch (start us, length us, event | category | flops | bytes accessed | tf_op | source)
XLA Modules:
  0.0 395.1 jit_solution(17090950568397289734)
XLA Ops:
  0.6 390.5 %exchange.1 = (bf16[64,256,128]{2,1,0:T(8,128)(2,1)S(1)}, bf16[64,256,128]{2,1,0:T(8,128)(2,1)S(1)}, bf16[4,4,2,2,16,128]{5,4,3,2,1,0:T(8,128)(2,1)S(1)}, f32[32,1,128]{2,1,0:T(1,128)S(1)}) custom-call(bf16[2,8192,128]{2,1,0:T(8,128)(2,1)} %k_hbm.1, bf16[2,8192,128]{2,1,0:T(8,128)(2,1)} %v_hbm.1, bf16[2,8,256,128]{3,2,1,0:T(8,128)(2,1)} %wq_hbm.1, ...), custom_call_target="tpu_custom_call" | custom-call | tf_op jit(solution)/shard_map/exchange/pallas_call | solution.py:365
  391.1 4.0 %write.1 = (bf16[64,256,128]{2,1,0:T(8,128)(2,1)}, bf16[64,256,128]{2,1,0:T(8,128)(2,1)}, bf16[4,4,2,2,16,128]{5,4,3,2,1,0:T(8,128)(2,1)}, f32[2,64]{1,0:T(2,128)}) custom-call(bf16[64,256,128]{2,1,0:T(8,128)(2,1)S(1)} %get-tuple-element.12.ck, bf16[64,256,128]{2,1,0:T(8,128)(2,1)S(1)} %get-tuple-element.13.cv, ...), custom_call_target="tpu_custom_call" | custom-call | tf_op jit(solution)/shard_map/write/pallas_call | solution.py:419

commit v2 on v1

--- a/solution.py
+++ b/solution.py
@@ -110,6 +110,8 @@
 
     pl.semaphore_wait(barrier, n - 1)
 
+    half = n // 2
+
     def send_share(src, dst, i, first, last):
         def one(turn, carry):
             step = jnp.where(turn % 2 == 0, (turn + 1) // 2, n - (turn + 1) // 2)
@@ -125,7 +127,8 @@
 
         lax.fori_loop(first, last, one, 0)
 
-    send_share(k_hbm, ck, 0, 1, n)
+    send_share(k_hbm, ck, 0, 1, half)
+    send_share(v_hbm, cv, 1, 1, half)
 
     for load in loads[:8]:
         load.wait()
@@ -201,8 +204,6 @@
 
         lax.fori_loop(0, chunks, mass_chunk, 0)
 
-    half = n // 2
-    send_share(v_hbm, cv, 1, half, n)
 
     def chip(step):
         return lax.rem(z + step + chips, chips) * 2 + c
@@ -215,6 +216,7 @@
     for copy in far:
         copy.start()
 
+    send_share(k_hbm, ck, 0, half, n)
     loads[8].wait()
     eye = lax.broadcasted_iota(jnp.int32, (blocks, blocks), 0) == lax.broadcasted_iota(
         jnp.int32, (blocks, blocks), 1
@@ -297,7 +299,7 @@
     keep_own = pltpu.make_async_copy(message.at[me], sco.at[me], own_sem.at[2])
     keep_own.start()
 
-    send_share(v_hbm, cv, 1, 1, half)
+    send_share(v_hbm, cv, 1, half, n)
 
     for copy in near:
         copy.wait()

time: 395 us -> 389 us (0.985); the launches traced: 395 us -> 383 us
  Pallas kernels: 395 us -> 382 us
    pallas_call x1, Pallas kernels: 391 us -> 378 us  [local(): pl.pallas_call(functools.partial(main_kernel, n), out_shape=[pltpu.VMEM((...]
where the time goes in v2:
time: 389 us; the launch traced here: 383 us
  Pallas kernels  382 us (98%)
    pallas_call x1, Pallas kernels, local(): pl.pallas_call(functools.partial(main_kernel, n), out_shape=[pltpu.VMEM((...  378 us

profile of v2, /device:TPU:324, one launch (start us, length us, event | category | flops | bytes accessed | tf_op | source)
XLA Modules:
  0.0 382.8 jit_solution(12413185886481595558)
XLA Ops:
  0.6 378.1 %exchange.1 = (bf16[64,256,128]{2,1,0:T(8,128)(2,1)S(1)}, bf16[64,256,128]{2,1,0:T(8,128)(2,1)S(1)}, bf16[4,4,2,2,16,128]{5,4,3,2,1,0:T(8,128)(2,1)S(1)}, f32[32,1,128]{2,1,0:T(1,128)S(1)}) custom-call(bf16[2,8192,128]{2,1,0:T(8,128)(2,1)} %k_hbm.1, bf16[2,8192,128]{2,1,0:T(8,128)(2,1)} %v_hbm.1, bf16[2,8,256,128]{3,2,1,0:T(8,128)(2,1)} %wq_hbm.1, ...), custom_call_target="tpu_custom_call" | custom-call | tf_op jit(solution)/shard_map/exchange/pallas_call | solution.py:367
  378.8 4.0 %write.1 = (bf16[64,256,128]{2,1,0:T(8,128)(2,1)}, bf16[64,256,128]{2,1,0:T(8,128)(2,1)}, bf16[4,4,2,2,16,128]{5,4,3,2,1,0:T(8,128)(2,1)}, f32[2,64]{1,0:T(2,128)}) custom-call(bf16[64,256,128]{2,1,0:T(8,128)(2,1)S(1)} %get-tuple-element.12.ck, bf16[64,256,128]{2,1,0:T(8,128)(2,1)S(1)} %get-tuple-element.13.cv, ...), custom_call_target="tpu_custom_call" | custom-call | tf_op jit(solution)/shard_map/write/pallas_call | solution.py:421

commit v3 on v2

--- a/solution.py
+++ b/solution.py
@@ -64,6 +64,7 @@
     recv_sem,
     small_send,
     small_recv,
+    met_sem,
 ):
     pairs, tokens, width = kbuf.shape
     share = tokens // n
@@ -80,10 +81,10 @@
     fold = scaling * LOG2E
 
     barrier = pltpu.get_barrier_semaphore()
-    for step in range(1, n):
-        pl.semaphore_signal(
-            barrier, inc=1, device_id={"seq": lax.rem(me + step, n)}, device_id_type=MESH
-        )
+    reach = n // 4
+    for step in range(reach, 0, -1):
+        for peer in (lax.rem(me + step, n), lax.rem(me + n - step, n)):
+            pl.semaphore_signal(barrier, inc=1, device_id={"seq": peer}, device_id_type=MESH)
 
     loads = [
         pltpu.make_async_copy(k_hbm, kbuf, load_sem.at[0]),
@@ -108,7 +109,9 @@
     for copy in own:
         copy.start()
 
-    pl.semaphore_wait(barrier, n - 1)
+    pl.semaphore_wait(barrier, 2 * reach)
+    for peer in (lax.rem(me + reach, n), lax.rem(me + n - reach, n)):
+        pl.semaphore_signal(met_sem, inc=1, device_id={"seq": peer}, device_id_type=MESH)
 
     half = n // 2
 
@@ -204,6 +207,8 @@
 
         lax.fori_loop(0, chunks, mass_chunk, 0)
 
+
+    pl.semaphore_wait(met_sem, 2)
 
     def chip(step):
         return lax.rem(z + step + chips, chips) * 2 + c
@@ -398,6 +403,7 @@
             pltpu.SemaphoreType.DMA((2,)),
             pltpu.SemaphoreType.DMA((8,)),
             pltpu.SemaphoreType.DMA((8,)),
+            pltpu.SemaphoreType.REGULAR,
         ],
         compiler_params=pltpu.CompilerParams(
             collective_id=0, has_side_effects=True, vmem_limit_bytes=36 * 1024 * 1024

time: 389 us -> 386 us (level); the launches traced: 383 us -> 386 us
  Pallas kernels: 382 us -> 386 us
where the time goes in v3:
time: 386 us
  Pallas kernels  386 us (100%)
    pallas_call x1, Pallas kernels, local(): pl.pallas_call(functools.partial(main_kernel, n), out_shape=[pltpu.VMEM((...  382 us

profile of v3, /device:TPU:324, one launch (start us, length us, event | category | flops | bytes accessed | tf_op | source)
XLA Modules:
  0.0 386.2 jit_solution(11045976319894788312)
XLA Ops:
  0.6 381.5 %exchange.1 = (bf16[64,256,128]{2,1,0:T(8,128)(2,1)S(1)}, bf16[64,256,128]{2,1,0:T(8,128)(2,1)S(1)}, bf16[4,4,2,2,16,128]{5,4,3,2,1,0:T(8,128)(2,1)S(1)}, f32[32,1,128]{2,1,0:T(1,128)S(1)}) custom-call(bf16[2,8192,128]{2,1,0:T(8,128)(2,1)} %k_hbm.1, bf16[2,8192,128]{2,1,0:T(8,128)(2,1)} %v_hbm.1, bf16[2,8,256,128]{3,2,1,0:T(8,128)(2,1)} %wq_hbm.1, ...), custom_call_target="tpu_custom_call" | custom-call | tf_op jit(solution)/shard_map/exchange/pallas_call | solution.py:372
  382.2 4.0 %write.1 = (bf16[64,256,128]{2,1,0:T(8,128)(2,1)}, bf16[64,256,128]{2,1,0:T(8,128)(2,1)}, bf16[4,4,2,2,16,128]{5,4,3,2,1,0:T(8,128)(2,1)}, f32[2,64]{1,0:T(2,128)}) custom-call(bf16[64,256,128]{2,1,0:T(8,128)(2,1)S(1)} %get-tuple-element.12.ck, bf16[64,256,128]{2,1,0:T(8,128)(2,1)S(1)} %get-tuple-element.13.cv, ...), custom_call_target="tpu_custom_call" | custom-call | tf_op jit(solution)/shard_map/write/pallas_call | solution.py:427
